TPU v7x, 256 devices: a whole 4x4x8 slice. The times are simulated.
256 devices in a mesh: south: 32 (over z, x), east: 8 (over y, core).
Axes of the slice: x: 4, y: 4, z: 8, core: 2. Of those that a mesh axis runs over, the one named last changes fastest.
Arguments:
- tracer: float32 [1024, 256, 128], P('south', 'east'), may hold values from 0.2 to 1.8
- flow_j: float32 [1024, 256, 128], P('south', 'east'), may hold values from -0.3 to 0.3
- flow_i: float32 [1024, 256, 128], P('south', 'east'), may hold values from -0.3 to 0.3
Outputs:
- running_total: float32 [1024, 256, 128], P('south', 'east')
- tracer_end: float32 [1024, 256, 128], P('south', 'east')
All inputs are finite; a program needn't handle non-finite values.
Results may differ from a plain program's by a relative error of at most 0.00002.
Values sent between devices are 32-bit elements; how exact they have to be, the bound alone decides.
No kernel may reach another device: no remote copies, remote signals or barrier semaphores. Data moves between devices by JAX's collectives and lax.ppermute only.
A program may use at most 64 MiB of HBM per device.

v0:
```python
import jax
import jax.numpy as jnp
from jax import lax
from jax.experimental import pallas as pl
from jax.experimental.pallas import tpu as pltpu
from jax.sharding import PartitionSpec as P


STEPS = 4
RATE = 0.05
TILE = 8
CHUNKS = 4
W = STEPS
CORNER = (W - 1, W - 2, W - 2)

VMEM = pl.BlockSpec(memory_space=pltpu.VMEM)
ANY = pl.BlockSpec(memory_space=pl.ANY)
HBM = pl.BlockSpec(memory_space=pltpu.HBM)


def exchange(array, partner):
    n_south, n_east = lax.axis_size("south"), lax.axis_size("east")
    pairs = []
    for i in range(n_south):
        for j in range(n_east):
            p, q = partner(i, j)
            pairs.append((i * n_east + j, p * n_east + q))
    return lax.ppermute(array, ("south", "east"), pairs)


def odd(i):
    return i + 1 if i % 2 else i - 1


def south_even(i, j):
    return i ^ 1, j


def south_odd(i, j):
    p = odd(i)
    inside = 0 <= p < lax.axis_size("south")
    return (p, j) if inside else (i, j ^ 1)


def east_even(i, j):
    return i, j ^ 1


def east_odd(i, j):
    q = odd(j)
    return i, q % lax.axis_size("east")


def call(kernel, outs, operands, in_specs, scratch=(), cost=0, aliases=None, result=(), out_specs=None):
    return pl.pallas_call(
        kernel,
        out_shape=tuple(
            (jax.ShapeDtypeStruct if i in result else pltpu.VMEM)(s, jnp.float32)
            for i, s in enumerate(outs)
        ),
        in_specs=in_specs,
        out_specs=out_specs or (VMEM,) * len(outs),
        scratch_shapes=scratch,
        compiler_params=pltpu.CompilerParams(vmem_limit_bytes=16 << 20),
        cost_estimate=pl.CostEstimate(flops=cost, bytes_accessed=cost, transcendentals=0),
        input_output_aliases=aliases or {},
    )(*operands)


def low_half(shape):
    return lax.broadcasted_iota(jnp.int32, shape, len(shape) - 2) < W


def place_of():
    south, east = lax.axis_index("south"), lax.axis_index("east")
    n_south, n_east = lax.axis_size("south"), lax.axis_size("east")
    conditions = (
        south % 2 == 0, east % 2 == 0, east < n_east - 1, east > 0, south > 0, south < n_south - 1
    )
    return tuple(c.astype(jnp.int32) for c in conditions)


def start_all(copies):
    for c in copies:
        c.start()
    return copies


def wait_all(copies):
    for c in copies:
        c.wait()


def pack_kernel(tracer, flow_j, flow_i, s0, s1, e0, e1, left, right, sems):
    rows, cols = tracer.shape[0], tracer.shape[1]
    even_s, even_e = place_of()[:2]
    arrays = (tracer, flow_j, flow_i)
    copies = []

    def copy(src, dst):
        c = pltpu.make_async_copy(src, dst, sems.at[len(copies)])
        c.start()
        copies.append(c)

    for k, a in enumerate(arrays):
        copy(a.at[:, pl.ds(0, TILE)], left.at[k])
        copy(a.at[:, pl.ds(cols - TILE, TILE)], right.at[k])
    at = 0
    for a, n in zip(arrays, (W, W - 1, W - 1)):
        high = rows - n
        copy(a.at[pl.ds(even_s * high, n)], s0.at[pl.ds(at, n)])
        copy(a.at[pl.ds((1 - even_s) * high, n)], s1.at[pl.ds(at, n)])
        at += n
    for c in copies[:6]:
        c.wait()
    half = rows // 2
    low = low_half((TILE, tracer.shape[2]))

    def fold(j, carry):
        for k in range(3):
            lo = jnp.where(low, left[k, j], pltpu.roll(left[k, j + half], W, 0))
            hi = jnp.where(low, pltpu.roll(right[k, j], W, 0), right[k, j + half])
            e0[k, j] = jnp.where(even_e == 1, hi, lo)
            e1[k, j] = jnp.where(even_e == 1, lo, hi)
        return carry

    lax.fori_loop(0, half, fold, 0, unroll=4)
    for c in copies[6:]:
        c.wait()


def unfolded(e0, e1, k, j):
    _, even_e, in_right, in_left, *_ = place_of()
    low = low_half(e0.shape[2:])
    gain = jnp.where(low, in_right, in_left).astype(jnp.float32)
    a, b = e0[k, j], e1[k, j]
    right = jnp.where(even_e == 1, a, b)
    left = jnp.where(even_e == 1, b, a)
    return (
        jnp.where(low, right, pltpu.roll(left, W, 0)) * gain,
        jnp.where(low, pltpu.roll(right, W, 0), left) * gain,
    )


def corner_kernel(e0, e1, c0, c1):
    half = e0.shape[1]
    even_s = place_of()[0]
    at = 0
    for k, depth in enumerate(CORNER):
        for d in range(depth):
            first = unfolded(e0, e1, k, d)[0]
            last = unfolded(e0, e1, k, half - 1 - d)[1]
            c0[at] = jnp.where(even_s == 1, last, first)
            c1[at] = jnp.where(even_s == 1, first, last)
            at += 1


def side_mask(shape):
    in_right, in_left = place_of()[2:4]
    return jnp.where(low_half(shape), in_right, in_left).astype(jnp.float32)


def advance(below, middle, above, flow_j, flow_i, mask):
    size, cols = middle.shape[0], middle.shape[0] - TILE
    right = pltpu.roll(middle, size - 1, 0)
    left = pltpu.roll(middle, 1, 0)
    spread = below + above + left + right - 4.0 * middle
    new = middle - flow_j * (above - below) - flow_i * (right - left) + RATE * spread
    return jnp.concatenate([new[:cols], new[cols:] * mask], axis=0)


def load_kernel(tracer, flow_j, flow_i, x, fj, fi, sems):
    cols = tracer.shape[1]
    wait_all(start_all([
        pltpu.make_async_copy(src, dst.at[:, pl.ds(0, cols)], sems.at[k])
        for k, (src, dst) in enumerate(((tracer, x), (flow_j, fj), (flow_i, fi)))
    ]))


def inner_kernel(e0, e1, x_in, fj_in, fi_in, x, fj, fi, kept, end, total):
    del x_in, fj_in, fi_in
    rows, cols = end.shape[0], end.shape[1]
    half = rows // 2

    def sides(j, carry):
        for k, dst in enumerate((x, fj, fi)):
            near, far = unfolded(e0, e1, k, j)
            dst[j, cols:] = near
            dst[half + j, cols:] = far
        return carry

    lax.fori_loop(0, half, sides, 0, unroll=4)
    mask = side_mask((TILE, x.shape[2]))

    for step in range(1, STEPS + 1):
        first, last = step, rows - 1 - step
        for n in range(2):
            kept[step - 1, 0, n] = x[first - 1 + n]
            kept[step - 1, 1, n] = x[last + 1 - n]

        def body(r, carry):
            below, middle = carry[:2]
            above = x[r + 1]
            new = advance(below, middle, above, fj[r], fi[r], mask)
            if step < STEPS:
                x[r] = new
                return middle, above
            end[r] = new[:cols]
            return middle, above, carry[2] + new[:cols]

        carry = (x[first - 1], x[first])
        if step == STEPS:
            carry += (jnp.zeros((cols, x.shape[2]), jnp.float32),)
        carry = lax.fori_loop(first, last + 1, body, carry, unroll=4)
    total[...] = carry[2]


def outer_kernel(
    recv0, recv1, corner0, corner1, fj, fi, kept, inner_end, inner_total, end, total
):
    del inner_end
    rows, cols = end.shape[0], end.shape[1]
    even_s, _, _, _, has_low, has_high = place_of()
    mask = side_mask((TILE, end.shape[2]))
    so_far = inner_total[...]

    for low in (True, False):
        ours = even_s == (0 if low else 1)
        gain = (has_low if low else has_high).astype(jnp.float32)

        def halo(at, k, d):
            row = jnp.where(ours, recv0[at], recv1[at])
            if d < CORNER[k]:
                n = sum(CORNER[:k]) + d
                side = jnp.where(ours, corner0[n], corner1[n])
            else:
                side = jnp.zeros_like(mask)
            return jnp.concatenate([row, side], axis=0)

        def at_edge(d, count):
            return count - 1 - d if low else d

        field = [halo(at_edge(d, W), 0, d) * gain for d in range(W)]
        flows = [
            [halo(base + at_edge(d, W - 1), k, d) for d in range(W - 1)]
            for k, base in ((1, W), (2, 2 * W - 1))
        ]

        def flow(k, own, at):
            row = at if low else rows - 1 - at
            return flows[k][-1 - at] if at < 0 else own[row]

        values = field[::-1]
        for step in range(1, STEPS + 1):
            side = 0 if low else 1
            inward = values + [kept[step - 1, side, 0], kept[step - 1, side, 1]]
            values = []
            for n in range(1, W + 1):
                at = n - 1 + step - W
                outside, middle, inside = inward[n - 1:n + 2]
                below, above = (outside, inside) if low else (inside, outside)
                new = advance(
                    below, middle, above, flow(0, fj, at), flow(1, fi, at), mask
                )
                values.append(new * gain if at < 0 else new)
        for at, value in enumerate(values):
            end[at if low else rows - 1 - at] = value[:cols]
            so_far = so_far + value[:cols]
    total[...] = so_far


def sums_kernel(scale, end, before, here, copied, running):
    carried = before[...] * scale

    def body(j, so_far):
        row = end[j]
        copied[j] = row
        so_far = so_far + row
        scaled = so_far * scale
        here[j] = scaled
        running[j] = scaled + carried
        return so_far

    lax.fori_loop(0, end.shape[0], body, jnp.zeros(end.shape[1:], jnp.float32), unroll=4)


def finish_kernel(scale, flip, here, before, other, partial, running, buffer, sems):
    del partial
    south = lax.axis_index("south")
    chunk = here.shape[0] // CHUNKS

    @pl.when((south ^ flip) < south)
    def _():
        carried = (before[...] + other[...]) * scale
        copies = []
        for n in range(CHUNKS):
            rows = pl.ds(n * chunk, chunk)
            buffer[rows] = here[rows] + carried
            copies.append(pltpu.make_async_copy(buffer.at[rows], running.at[rows], sems.at[n]))
            copies[-1].start()
        wait_all(copies)


def per_device(tracer, flow_j, flow_i):
    rows, cols, members = tracer.shape
    south = lax.axis_index("south")
    n_south = lax.axis_size("south")
    fields = tuple(pltpu.with_memory_space_constraint(a, pltpu.HBM) for a in (tracer, flow_j, flow_i))
    edge = (3 * W - 2, cols, members)
    fold = (3, rows // 2, TILE, members)
    s0, s1, e0, e1 = call(
        pack_kernel, (edge, edge, fold, fold), fields, [HBM] * 3,
        [pltpu.VMEM((3, rows, TILE, members), jnp.float32)] * 2 + [pltpu.SemaphoreType.DMA((12,))],
    )
    e1 = exchange(e1, east_odd)
    e0 = exchange(e0, east_even)
    s1 = exchange(s1, south_odd)
    s0 = exchange(s0, south_even)

    corner = (sum(CORNER), TILE, members)
    c0, c1 = call(corner_kernel, (corner, corner), (e0, e1), [VMEM] * 2)
    c1 = exchange(c1, south_odd)
    c0 = exchange(c0, south_even)

    wide = (rows, cols + TILE, members)
    ends = (STEPS, 2, 2, cols + TILE, members)
    loaded = call(
        load_kernel, (wide,) * 3, fields, [HBM] * 3, [pltpu.SemaphoreType.DMA((3,))],
        cost=1 << 22,
    )
    _, *inner = call(
        inner_kernel, (wide,) * 3 + (ends, tracer.shape, (cols, members)),
        (e0, e1, *loaded), [VMEM] * 5, cost=1 << 22, aliases={2: 0, 3: 1, 4: 2},
    )
    end, total = call(
        outer_kernel, (tracer.shape, (cols, members)), (s0, s1, c0, c1, *inner),
        [VMEM] * 9, aliases={7: 0},
    )
    scale = 1.0 / (rows * n_south)

    before = jnp.zeros_like(total)
    for flips in ((1, 3, 2), (4, 12, 8)):
        parts = [exchange(total, lambda i, j, k=k: (i ^ k, j)) for k in flips]
        for k, part in zip(flips, parts):
            before = before + jnp.where((south ^ k) < south, part, 0.0)
        total = total + sum(parts)
    flip = 28
    other = exchange(total, lambda i, j: (i ^ flip, j))

    here, end, running_total = call(
        lambda *refs: sums_kernel(scale, *refs), (tracer.shape,) * 3, (end, before),
        [VMEM] * 2, cost=1 << 21, result=(1, 2),
    )
    (running_total,) = call(
        lambda *refs: finish_kernel(scale, flip, *refs), (tracer.shape,),
        (here, before, other, pltpu.with_memory_space_constraint(running_total, pltpu.HBM)),
        [VMEM] * 3 + [HBM],
        [pltpu.VMEM(tracer.shape, jnp.float32), pltpu.SemaphoreType.DMA((CHUNKS,))],
        aliases={3: 0}, result=(0,), out_specs=(HBM,),
    )
    return running_total, end


def solution(mesh):
    spec = P("south", "east", None)
    return jax.shard_map(
        per_device, mesh=mesh, in_specs=(spec,) * 3, out_specs=(spec,) * 2, check_vma=False
    )
```

profile of v0, /device:TPU:64, one launch (start us, length us, event | category | flops | bytes accessed | tf_op | source)
XLA Modules:
  0.0 40.7 jit_solution(3982435013585804095)
XLA Ops:
  0.6 1.4 %shard_map.50 = (f32[10,32,128]{2,1,0:T(8,128)S(1)}, f32[10,32,128]{2,1,0:T(8,128)S(1)}, f32[3,16,8,128]{3,2,1,0:T(8,128)S(1)}, f32[3,16,8,128]{3,2,1,0:T(8,128)S(1)}) custom-call(f32[32,32,128]{2,1,0:T(8,128)} %tracer.3, f32[32,32,128]{2,1,0:T(8,128)} %flow_j.3, f32[32,32,128]{2,1,0:T(8,128)} %flow_i.3), custom_call_target="tpu_custom_call" | custom-call | tf_op jit(solution)/shard_map/pallas_call | solution.py:55
  2.0 0.1 collective-permute-start.2
  2.1 3.1 %collective-permute-start.3 = (f32[3,16,8,128]{3,2,1,0:T(8,128)S(1)}, f32[3,16,8,128]{3,2,1,0:T(8,128)S(1)}, u32[]{:S(2)}, u32[]{:S(2)}) collective-permute-start(f32[3,16,8,128]{3,2,1,0:T(8,128)S(1)} %get-tuple-element.24), channel_id=1, source_target_pairs={{0,7},{1,2},{2,1},{3,4},{4,3},{5,6},{6,5},{7,0},{8,15},{9,10},{10,... | collective-permute-start | bytes 589832 | tf_op jit(solution)/shard_map/ppermute | solution.py:28
  5.2 1.5 %collective-permute-start = (f32[10,32,128]{2,1,0:T(8,128)S(1)}, f32[10,32,128]{2,1,0:T(8,128)S(1)}, u32[]{:S(2)}, u32[]{:S(2)}) collective-permute-start(f32[10,32,128]{2,1,0:T(8,128)S(1)} %get-tuple-element.21), channel_id=1, source_target_pairs={{0,8},{1,9},{2,10},{3,11},{4,12},{5,13},{6,14},{7,15},{8,0},{9,1},... | collective-permute-start | bytes 491528 | tf_op jit(solution)/shard_map/ppermute | solution.py:28
  6.7 1.6 %collective-permute-start.1 = (f32[10,32,128]{2,1,0:T(8,128)S(1)}, f32[10,32,128]{2,1,0:T(8,128)S(1)}, u32[]{:S(2)}, u32[]{:S(2)}) collective-permute-start(f32[10,32,128]{2,1,0:T(8,128)S(1)} %get-tuple-element.22), channel_id=1, source_target_pairs={{0,1},{1,0},{2,3},{3,2},{4,5},{5,4},{6,7},{7,6},{8,16},{9,17},{10,... | collective-permute-start | bytes 491528 | tf_op jit(solution)/shard_map/ppermute | solution.py:28
  8.4 0.0 collective-permute-done.2.e0
  8.4 0.2 collective-permute-done.3.e1
  8.6 1.6 %collective-permute-start.4 = (f32[7,8,128]{2,1,0:T(8,128)S(1)}, f32[7,8,128]{2,1,0:T(8,128)S(1)}, u32[]{:S(2)}, u32[]{:S(2)}) collective-permute-start(f32[7,8,128]{2,1,0:T(8,128)S(1)} %get-tuple-element.25), channel_id=1, source_target_pairs={{0,8},{1,9},{2,10},{3,11},{4,12},{5,13},{6,14},{7,15},{8,0},{9,1},... | collective-permute-start | bytes 86024 | tf_op jit(solution)/shard_map/ppermute | solution.py:28
  10.2 1.6 %collective-permute-start.5 = (f32[7,8,128]{2,1,0:T(8,128)S(1)}, f32[7,8,128]{2,1,0:T(8,128)S(1)}, u32[]{:S(2)}, u32[]{:S(2)}) collective-permute-start(f32[7,8,128]{2,1,0:T(8,128)S(1)} %get-tuple-element.26), channel_id=1, source_target_pairs={{0,1},{1,0},{2,3},{3,2},{4,5},{5,4},{6,7},{7,6},{8,16},{9,17},{10,... | collective-permute-start | bytes 86024 | tf_op jit(solution)/shard_map/ppermute | solution.py:28
  11.8 1.4 %shard_map.52 = (f32[32,40,128]{2,1,0:T(8,128)S(1)}, f32[32,40,128]{2,1,0:T(8,128)S(1)}, f32[32,40,128]{2,1,0:T(8,128)S(1)}) custom-call(f32[32,32,128]{2,1,0:T(8,128)} %tracer.3, f32[32,32,128]{2,1,0:T(8,128)} %flow_j.3, f32[32,32,128]{2,1,0:T(8,128)} %flow_i.3), custom_call_target="tpu_custom_call" | custom-call | flops 4194304 | bytes 4194304 | tf_op jit(solution)/shard_map/pallas_call | solution.py:55
  13.2 1.5 %shard_map.53 = (f32[32,40,128]{2,1,0:T(8,128)S(1)}, f32[32,40,128]{2,1,0:T(8,128)S(1)}, f32[32,40,128]{2,1,0:T(8,128)S(1)}, f32[4,2,2,40,128]{4,3,2,1,0:T(8,128...) custom-call(f32[3,16,8,128]{3,2,1,0:T(8,128)S(1)} %collective-permut, ...), custom_call_target="tpu_custom_call", output_to_operand_aliasing={{0}: (2, {}), {1}: (3, {}), {2}: (4, {})} | custom-call | flops 4194304 | bytes 4194304 | tf_op jit(solution)/shard_map/pallas_call | solution.py:55
  14.7 0.0 collective-permute-done.recv0
  14.7 0.0 collective-permute-done.1.recv1
  14.8 0.0 collective-permute-done.4.corner0
  14.8 1.4 %collective-permute-done.5.corner1 = f32[7,8,128]{2,1,0:T(8,128)S(1)} collective-permute-done((f32[7,8,128]{2,1,0:T(8,128)S(1)}, f32[7,8,128]{2,1,0:T(8,128)S(1)}, u32[]{:S(2)}, u32[]{:S(2)}) %collective-permute-start.5) | collective-permute-done | bytes 28704 | tf_op jit(solution)/shard_map/ppermute | solution.py:28
  16.2 0.4 shard_map.54
  16.6 0.1 collective-permute-start.6
  16.7 2.2 %collective-permute-start.7 = (f32[32,128]{1,0:T(8,128)S(1)}, f32[32,128]{1,0:T(8,128)S(1)}, u32[]{:S(2)}, u32[]{:S(2)}) collective-permute-start(f32[32,128]{1,0:T(8,128)S(1)} %get-tuple-element.36), channel_id=1, source_target_pairs={{0,24},{1,25},{2,26},{3,27},{4,28},{5,29},{6,30},{7,31},{8,16},{9,... | collective-permute-start | bytes 49160 | tf_op jit(solution)/shard_map/ppermute | solution.py:28
  18.9 1.9 %collective-permute-start.8 = (f32[32,128]{1,0:T(8,128)S(1)}, f32[32,128]{1,0:T(8,128)S(1)}, u32[]{:S(2)}, u32[]{:S(2)}) collective-permute-start(f32[32,128]{1,0:T(8,128)S(1)} %get-tuple-element.36), channel_id=1, source_target_pairs={{0,16},{1,17},{2,18},{3,19},{4,20},{5,21},{6,22},{7,23},{8,24},{9,... | collective-permute-start | bytes 49160 | tf_op jit(solution)/shard_map/ppermute | solution.py:28
  20.8 0.0 collective-permute-done.6
  20.8 1.0 %collective-permute-done.7 = f32[32,128]{1,0:T(8,128)S(1)} collective-permute-done((f32[32,128]{1,0:T(8,128)S(1)}, f32[32,128]{1,0:T(8,128)S(1)}, u32[]{:S(2)}, u32[]{:S(2)}) %collective-permute-start.7) | collective-permute-done | bytes 16416 | tf_op jit(solution)/shard_map/ppermute | solution.py:28
  21.7 2.4 %collective-permute-done.8 = f32[32,128]{1,0:T(8,128)S(1)} collective-permute-done((f32[32,128]{1,0:T(8,128)S(1)}, f32[32,128]{1,0:T(8,128)S(1)}, u32[]{:S(2)}, u32[]{:S(2)}) %collective-permute-start.8) | collective-permute-done | bytes 16416 | tf_op jit(solution)/shard_map/ppermute | solution.py:28
  24.1 0.1 collective-permute-start.10
  24.2 5.9 %collective-permute-start.11 = (f32[32,128]{1,0:T(8,128)S(1)}, f32[32,128]{1,0:T(8,128)S(1)}, u32[]{:S(2)}, u32[]{:S(2)}) collective-permute-start(f32[32,128]{1,0:T(8,128)S(1)} %add_add_fusion.1), channel_id=1, source_target_pairs={{0,64},{1,65},{2,66},{3,67},{4,68},{5,69},{6,70},{7,71},{8,72},{9,... | collective-permute-start | bytes 49160 | tf_op jit(solution)/shard_map/ppermute | solution.py:28
  30.1 0.0 collective-permute-start.9
  30.1 0.0 collective-permute-done.10
  30.1 1.9 %collective-permute-done.11 = f32[32,128]{1,0:T(8,128)S(1)} collective-permute-done((f32[32,128]{1,0:T(8,128)S(1)}, f32[32,128]{1,0:T(8,128)S(1)}, u32[]{:S(2)}, u32[]{:S(2)}) %collective-permute-start.11) | collective-permute-done | bytes 16416 | tf_op jit(solution)/shard_map/ppermute | solution.py:28
  32.0 1.9 %collective-permute-done.9 = f32[32,128]{1,0:T(8,128)S(1)} collective-permute-done((f32[32,128]{1,0:T(8,128)S(1)}, f32[32,128]{1,0:T(8,128)S(1)}, u32[]{:S(2)}, u32[]{:S(2)}) %collective-permute-start.9) | collective-permute-done | bytes 16416 | tf_op jit(solution)/shard_map/ppermute | solution.py:28
  33.8 2.4 %collective-permute-start.12 = (f32[32,128]{1,0:T(8,128)S(1)}, f32[32,128]{1,0:T(8,128)S(1)}, u32[]{:S(2)}, u32[]{:S(2)}) collective-permute-start(f32[32,128]{1,0:T(8,128)S(1)} %get-tuple-element.40), channel_id=1, source_target_pairs={{0,224},{1,225},{2,226},{3,227},{4,228},{5,229},{6,230},{7,231},{8... | collective-permute-start | bytes 49160 | tf_op jit(solution)/shard_map/ppermute | solution.py:28
  36.3 1.1 %shard_map.55 = (f32[32,32,128]{2,1,0:T(8,128)S(1)}, f32[32,32,128]{2,1,0:T(8,128)}, f32[32,32,128]{2,1,0:T(8,128)}) custom-call(f32[32,32,128]{2,1,0:T(8,128)S(1)} %get-tuple-element.35.refs_0_, f32[32,128]{1,0:T(8,128)S(1)} %get-tuple-element.41.refs_1_), custom_call_target="tpu_custom_call" | custom-call | flops 2097152 | bytes 2097152 | tf_op jit(solution)/shard_map/pallas_call | solution.py:55
  37.3 3.3 %collective-permute-done.12.refs_2_ = f32[32,128]{1,0:T(8,128)S(1)} collective-permute-done((f32[32,128]{1,0:T(8,128)S(1)}, f32[32,128]{1,0:T(8,128)S(1)}, u32[]{:S(2)}, u32[]{:S(2)}) %collective-permute-start.12) | collective-permute-done | bytes 16416 | tf_op jit(solution)/shard_map/ppermute | solution.py:28
  (4 shorter events, 0.1 us)
Async XLA Ops:
  2.0 6.4 %collective-permute-start.2 = (f32[3,16,8,128]{3,2,1,0:T(8,128)S(1)}, f32[3,16,8,128]{3,2,1,0:T(8,128)S(1)}, u32[]{:S(2)}, u32[]{:S(2)}) collective-permute-start(f32[3,16,8,128]{3,2,1,0:T(8,128)S(1)} %get-tuple-element.23), channel_id=1, source_target_pairs={{0,1},{1,0},{2,3},{3,2},{4,5},{5,4},{6,7},{7,6},{8,9},{9,8},{10,11... | collective-permute-start | bytes 589832 | tf_op jit(solution)/shard_map/ppermute | solution.py:28
  2.1 6.5 %collective-permute-start.3 = (f32[3,16,8,128]{3,2,1,0:T(8,128)S(1)}, f32[3,16,8,128]{3,2,1,0:T(8,128)S(1)}, u32[]{:S(2)}, u32[]{:S(2)}) collective-permute-start(f32[3,16,8,128]{3,2,1,0:T(8,128)S(1)} %get-tuple-element.24), channel_id=1, source_target_pairs={{0,7},{1,2},{2,1},{3,4},{4,3},{5,6},{6,5},{7,0},{8,15},{9,10},{10,... | collective-permute-start | bytes 589832 | tf_op jit(solution)/shard_map/ppermute | solution.py:28
  5.2 9.5 %collective-permute-start = (f32[10,32,128]{2,1,0:T(8,128)S(1)}, f32[10,32,128]{2,1,0:T(8,128)S(1)}, u32[]{:S(2)}, u32[]{:S(2)}) collective-permute-start(f32[10,32,128]{2,1,0:T(8,128)S(1)} %get-tuple-element.21), channel_id=1, source_target_pairs={{0,8},{1,9},{2,10},{3,11},{4,12},{5,13},{6,14},{7,15},{8,0},{9,1},... | collective-permute-start | bytes 491528 | tf_op jit(solution)/shard_map/ppermute | solution.py:28
  6.7 8.0 %collective-permute-start.1 = (f32[10,32,128]{2,1,0:T(8,128)S(1)}, f32[10,32,128]{2,1,0:T(8,128)S(1)}, u32[]{:S(2)}, u32[]{:S(2)}) collective-permute-start(f32[10,32,128]{2,1,0:T(8,128)S(1)} %get-tuple-element.22), channel_id=1, source_target_pairs={{0,1},{1,0},{2,3},{3,2},{4,5},{5,4},{6,7},{7,6},{8,16},{9,17},{10,... | collective-permute-start | bytes 491528 | tf_op jit(solution)/shard_map/ppermute | solution.py:28
  8.6 6.1 %collective-permute-start.4 = (f32[7,8,128]{2,1,0:T(8,128)S(1)}, f32[7,8,128]{2,1,0:T(8,128)S(1)}, u32[]{:S(2)}, u32[]{:S(2)}) collective-permute-start(f32[7,8,128]{2,1,0:T(8,128)S(1)} %get-tuple-element.25), channel_id=1, source_target_pairs={{0,8},{1,9},{2,10},{3,11},{4,12},{5,13},{6,14},{7,15},{8,0},{9,1},... | collective-permute-start | bytes 86024 | tf_op jit(solution)/shard_map/ppermute | solution.py:28
  10.2 6.0 %collective-permute-start.5 = (f32[7,8,128]{2,1,0:T(8,128)S(1)}, f32[7,8,128]{2,1,0:T(8,128)S(1)}, u32[]{:S(2)}, u32[]{:S(2)}) collective-permute-start(f32[7,8,128]{2,1,0:T(8,128)S(1)} %get-tuple-element.26), channel_id=1, source_target_pairs={{0,1},{1,0},{2,3},{3,2},{4,5},{5,4},{6,7},{7,6},{8,16},{9,17},{10,... | collective-permute-start | bytes 86024 | tf_op jit(solution)/shard_map/ppermute | solution.py:28
  16.6 4.2 %collective-permute-start.6 = (f32[32,128]{1,0:T(8,128)S(1)}, f32[32,128]{1,0:T(8,128)S(1)}, u32[]{:S(2)}, u32[]{:S(2)}) collective-permute-start(f32[32,128]{1,0:T(8,128)S(1)} %get-tuple-element.36), channel_id=1, source_target_pairs={{0,8},{1,9},{2,10},{3,11},{4,12},{5,13},{6,14},{7,15},{8,0},{9,1},... | collective-permute-start | bytes 49160 | tf_op jit(solution)/shard_map/ppermute | solution.py:28
  16.7 5.0 %collective-permute-start.7 = (f32[32,128]{1,0:T(8,128)S(1)}, f32[32,128]{1,0:T(8,128)S(1)}, u32[]{:S(2)}, u32[]{:S(2)}) collective-permute-start(f32[32,128]{1,0:T(8,128)S(1)} %get-tuple-element.36), channel_id=1, source_target_pairs={{0,24},{1,25},{2,26},{3,27},{4,28},{5,29},{6,30},{7,31},{8,16},{9,... | collective-permute-start | bytes 49160 | tf_op jit(solution)/shard_map/ppermute | solution.py:28
  18.9 5.2 %collective-permute-start.8 = (f32[32,128]{1,0:T(8,128)S(1)}, f32[32,128]{1,0:T(8,128)S(1)}, u32[]{:S(2)}, u32[]{:S(2)}) collective-permute-start(f32[32,128]{1,0:T(8,128)S(1)} %get-tuple-element.36), channel_id=1, source_target_pairs={{0,16},{1,17},{2,18},{3,19},{4,20},{5,21},{6,22},{7,23},{8,24},{9,... | collective-permute-start | bytes 49160 | tf_op jit(solution)/shard_map/ppermute | solution.py:28
  24.1 6.0 %collective-permute-start.10 = (f32[32,128]{1,0:T(8,128)S(1)}, f32[32,128]{1,0:T(8,128)S(1)}, u32[]{:S(2)}, u32[]{:S(2)}) collective-permute-start(f32[32,128]{1,0:T(8,128)S(1)} %add_add_fusion.1), channel_id=1, source_target_pairs={{0,96},{1,97},{2,98},{3,99},{4,100},{5,101},{6,102},{7,103},{8,104... | collective-permute-start | bytes 49160 | tf_op jit(solution)/shard_map/ppermute | solution.py:28
  24.2 7.7 %collective-permute-start.11 = (f32[32,128]{1,0:T(8,128)S(1)}, f32[32,128]{1,0:T(8,128)S(1)}, u32[]{:S(2)}, u32[]{:S(2)}) collective-permute-start(f32[32,128]{1,0:T(8,128)S(1)} %add_add_fusion.1), channel_id=1, source_target_pairs={{0,64},{1,65},{2,66},{3,67},{4,68},{5,69},{6,70},{7,71},{8,72},{9,... | collective-permute-start | bytes 49160 | tf_op jit(solution)/shard_map/ppermute | solution.py:28
  30.1 3.7 %collective-permute-start.9 = (f32[32,128]{1,0:T(8,128)S(1)}, f32[32,128]{1,0:T(8,128)S(1)}, u32[]{:S(2)}, u32[]{:S(2)}) collective-permute-start(f32[32,128]{1,0:T(8,128)S(1)} %add_add_fusion.1), channel_id=1, source_target_pairs={{0,32},{1,33},{2,34},{3,35},{4,36},{5,37},{6,38},{7,39},{8,40},{9,... | collective-permute-start | bytes 49160 | tf_op jit(solution)/shard_map/ppermute | solution.py:28
  33.8 6.8 %collective-permute-start.12 = (f32[32,128]{1,0:T(8,128)S(1)}, f32[32,128]{1,0:T(8,128)S(1)}, u32[]{:S(2)}, u32[]{:S(2)}) collective-permute-start(f32[32,128]{1,0:T(8,128)S(1)} %get-tuple-element.40), channel_id=1, source_target_pairs={{0,224},{1,225},{2,226},{3,227},{4,228},{5,229},{6,230},{7,231},{8... | collective-permute-start | bytes 49160 | tf_op jit(solution)/shard_map/ppermute | solution.py:28
where the time goes:
time: 40.8 us; the launch traced here: 40.7 us
  starting transfers between devices  22.1 us (54%)
  waiting for transfers between devices  12 us (29%)
  Pallas kernels  5.8 us (14%)
  between operations  0.71 us (2%)
    ppermute x13, starting transfers between devices, exchange(): return lax.ppermute(array, ('south', 'east'), pairs)  22.1 us
    ppermute x13, waiting for transfers between devices, exchange(): return lax.ppermute(array, ('south', 'east'), pairs)  12 us
    pallas_call x7, Pallas kernels, call(): pl.pallas_call(kernel, out_shape=tuple(((jax.ShapeDtypeStruct if i in res...  5.8 us
  transfers between devices with their start and end apart: 13, of which 7 were waited for; matrix products, arithmetic and copies ran while one was open for 0% of the time, Pallas kernels for 10%

commit v1 on v0

--- a/solution.py
+++ b/solution.py
@@ -48,7 +48,8 @@
 
 def east_odd(i, j):
     q = odd(j)
-    return i, q % lax.axis_size("east")
+    inside = 0 <= q < lax.axis_size("east")
+    return (i, q) if inside else (i ^ 1, j)
 
 
 def call(kernel, outs, operands, in_specs, scratch=(), cost=0, aliases=None, result=(), out_specs=None):
@@ -169,18 +170,13 @@
     return jnp.concatenate([new[:cols], new[cols:] * mask], axis=0)
 
 
-def load_kernel(tracer, flow_j, flow_i, x, fj, fi, sems):
-    cols = tracer.shape[1]
-    wait_all(start_all([
+def inner_kernel(tracer, flow_j, flow_i, e0, e1, fj, fi, kept, end, total, x, sems):
+    rows, cols = end.shape[0], end.shape[1]
+    half = rows // 2
+    copies = start_all([
         pltpu.make_async_copy(src, dst.at[:, pl.ds(0, cols)], sems.at[k])
         for k, (src, dst) in enumerate(((tracer, x), (flow_j, fj), (flow_i, fi)))
-    ]))
-
-
-def inner_kernel(e0, e1, x_in, fj_in, fi_in, x, fj, fi, kept, end, total):
-    del x_in, fj_in, fi_in
-    rows, cols = end.shape[0], end.shape[1]
-    half = rows // 2
+    ])
 
     def sides(j, carry):
         for k, dst in enumerate((x, fj, fi)):
@@ -190,6 +186,7 @@
         return carry
 
     lax.fori_loop(0, half, sides, 0, unroll=4)
+    wait_all(copies)
     mask = side_mask((TILE, x.shape[2]))
 
     for step in range(1, STEPS + 1):
@@ -324,13 +321,10 @@
 
     wide = (rows, cols + TILE, members)
     ends = (STEPS, 2, 2, cols + TILE, members)
-    loaded = call(
-        load_kernel, (wide,) * 3, fields, [HBM] * 3, [pltpu.SemaphoreType.DMA((3,))],
-        cost=1 << 22,
-    )
-    _, *inner = call(
-        inner_kernel, (wide,) * 3 + (ends, tracer.shape, (cols, members)),
-        (e0, e1, *loaded), [VMEM] * 5, cost=1 << 22, aliases={2: 0, 3: 1, 4: 2},
+    inner = call(
+        inner_kernel, (wide, wide, ends, tracer.shape, (cols, members)),
+        (tracer, flow_j, flow_i, e0, e1), [ANY] * 3 + [VMEM] * 2,
+        [pltpu.VMEM(wide, jnp.float32), pltpu.SemaphoreType.DMA((3,))], cost=1 << 22,
     )
     end, total = call(
         outer_kernel, (tracer.shape, (cols, members)), (s0, s1, c0, c1, *inner),

time: 40.8 us -> 41.1 us (level)
  waiting for transfers between devices: 12 us -> 15.1 us
  starting transfers between devices: 22.1 us -> 20.5 us
  Pallas kernels: 5.8 us -> 4.69 us
    ppermute x13, waiting for transfers between devices: 12 us -> 15.1 us  [exchange(): return lax.ppermute(array, ('south', 'east'), pairs)]
    ppermute x13, starting transfers between devices: 22.1 us -> 20.5 us  [exchange(): return lax.ppermute(array, ('south', 'east'), pairs)]
    pallas_call x7 -> x6, Pallas kernels: 5.8 us -> 4.69 us  [call(): pl.pallas_call(kernel, out_shape=tuple(((jax.ShapeDtypeStruct if i in res...]
  transfers between devices with their start and end apart: 13 -> 13, of which waited for: 7 -> 7; matrix products, arithmetic and copies ran while one was open for 0% -> 0% of each run, Pallas kernels for 10% -> 7%
where the time goes in v1:
time: 41.1 us; the launch traced here: 41 us
  starting transfers between devices  20.5 us (50%)
  waiting for transfers between devices  15.1 us (37%)
  Pallas kernels  4.69 us (11%)
  between operations  0.73 us (2%)
    ppermute x13, starting transfers between devices, exchange(): return lax.ppermute(array, ('south', 'east'), pairs)  20.5 us
    ppermute x13, waiting for transfers between devices, exchange(): return lax.ppermute(array, ('south', 'east'), pairs)  15.1 us
    pallas_call x6, Pallas kernels, call(): pl.pallas_call(kernel, out_shape=tuple(((jax.ShapeDtypeStruct if i in res...  4.69 us
  transfers between devices with their start and end apart: 13, of which 7 were waited for; matrix products, arithmetic and copies ran while one was open for 0% of the time, Pallas kernels for 7%

profile of v1, /device:TPU:64, one launch (start us, length us, event | category | flops | bytes accessed | tf_op | source)
XLA Modules:
  0.0 41.0 jit_solution(12178060520050795563)
XLA Ops:
  0.6 0.0 copy-start
  0.6 0.0 copy-start.1
  0.7 1.5 %shard_map.50 = (f32[10,32,128]{2,1,0:T(8,128)S(1)}, f32[10,32,128]{2,1,0:T(8,128)S(1)}, f32[3,16,8,128]{3,2,1,0:T(8,128)S(1)}, f32[3,16,8,128]{3,2,1,0:T(8,128)S(1)}) custom-call(f32[32,32,128]{2,1,0:T(8,128)} %tracer.3, f32[32,32,128]{2,1,0:T(8,128)} %flow_j.3, f32[32,32,128]{2,1,0:T(8,128)} %flow_i.3), custom_call_target="tpu_custom_call" | custom-call | tf_op jit(solution)/shard_map/pallas_call | solution.py:56
  2.2 0.1 collective-permute-start.2
  2.3 1.6 %collective-permute-start.3 = (f32[3,16,8,128]{3,2,1,0:T(8,128)S(1)}, f32[3,16,8,128]{3,2,1,0:T(8,128)S(1)}, u32[]{:S(2)}, u32[]{:S(2)}) collective-permute-start(f32[3,16,8,128]{3,2,1,0:T(8,128)S(1)} %get-tuple-element.21), channel_id=1, source_target_pairs={{0,8},{1,2},{2,1},{3,4},{4,3},{5,6},{6,5},{7,15},{8,0},{9,10},{10,... | collective-permute-start | bytes 589832 | tf_op jit(solution)/shard_map/ppermute | solution.py:28
  3.8 0.5 %collective-permute-start = (f32[10,32,128]{2,1,0:T(8,128)S(1)}, f32[10,32,128]{2,1,0:T(8,128)S(1)}, u32[]{:S(2)}, u32[]{:S(2)}) collective-permute-start(f32[10,32,128]{2,1,0:T(8,128)S(1)} %get-tuple-element.18), channel_id=1, source_target_pairs={{0,8},{1,9},{2,10},{3,11},{4,12},{5,13},{6,14},{7,15},{8,0},{9,1},... | collective-permute-start | bytes 491528 | tf_op jit(solution)/shard_map/ppermute | solution.py:28
  4.4 2.3 %collective-permute-start.1 = (f32[10,32,128]{2,1,0:T(8,128)S(1)}, f32[10,32,128]{2,1,0:T(8,128)S(1)}, u32[]{:S(2)}, u32[]{:S(2)}) collective-permute-start(f32[10,32,128]{2,1,0:T(8,128)S(1)} %get-tuple-element.19), channel_id=1, source_target_pairs={{0,1},{1,0},{2,3},{3,2},{4,5},{5,4},{6,7},{7,6},{8,16},{9,17},{10,... | collective-permute-start | bytes 491528 | tf_op jit(solution)/shard_map/ppermute | solution.py:28
  6.7 0.0 collective-permute-done.2.e0
  6.7 2.7 %collective-permute-done.3.e1 = f32[3,16,8,128]{3,2,1,0:T(8,128)S(1)} collective-permute-done((f32[3,16,8,128]{3,2,1,0:T(8,128)S(1)}, f32[3,16,8,128]{3,2,1,0:T(8,128)S(1)}, u32[]{:S(2)}, u32[]{:S(2)}) %collective-permute-start.3) | collective-permute-done | bytes 196640 | tf_op jit(solution)/shard_map/ppermute | solution.py:28
  9.4 1.6 %collective-permute-start.4 = (f32[7,8,128]{2,1,0:T(8,128)S(1)}, f32[7,8,128]{2,1,0:T(8,128)S(1)}, u32[]{:S(2)}, u32[]{:S(2)}) collective-permute-start(f32[7,8,128]{2,1,0:T(8,128)S(1)} %get-tuple-element.22), channel_id=1, source_target_pairs={{0,8},{1,9},{2,10},{3,11},{4,12},{5,13},{6,14},{7,15},{8,0},{9,1},... | collective-permute-start | bytes 86024 | tf_op jit(solution)/shard_map/ppermute | solution.py:28
  11.0 1.6 %collective-permute-start.5 = (f32[7,8,128]{2,1,0:T(8,128)S(1)}, f32[7,8,128]{2,1,0:T(8,128)S(1)}, u32[]{:S(2)}, u32[]{:S(2)}) collective-permute-start(f32[7,8,128]{2,1,0:T(8,128)S(1)} %get-tuple-element.23), channel_id=1, source_target_pairs={{0,1},{1,0},{2,3},{3,2},{4,5},{5,4},{6,7},{7,6},{8,16},{9,17},{10,... | collective-permute-start | bytes 86024 | tf_op jit(solution)/shard_map/ppermute | solution.py:28
  12.7 1.7 %shard_map.52 = (f32[32,40,128]{2,1,0:T(8,128)S(1)}, f32[32,40,128]{2,1,0:T(8,128)S(1)}, f32[4,2,2,40,128]{4,3,2,1,0:T(8,128)S(1)}, f32[32,32,128]{2,1,0:T(8,128)S(1)}, f32[32,128]{1,0:T(8,128)S(1)}) custom-call(f32[32,32,128]{2,1,0:T(8,128)S(1)} %copy-done, f32[32,32,128]{2,1,0:T(8,128)S(1)} %copy-done.1, f32[32,32,128]{2,1,0:T(8,128)S(1)} %copy-done.2, ...), custom_call_target="tpu_custom_call" | custom-call | flops 4194304 | bytes 4194304 | tf_op jit(solution)/shard_map/pallas_call | solution.py:56
  14.3 0.0 collective-permute-done.recv0
  14.3 0.0 collective-permute-done.1.recv1
  14.3 0.0 collective-permute-done.4.corner0
  14.3 2.6 %collective-permute-done.5.corner1 = f32[7,8,128]{2,1,0:T(8,128)S(1)} collective-permute-done((f32[7,8,128]{2,1,0:T(8,128)S(1)}, f32[7,8,128]{2,1,0:T(8,128)S(1)}, u32[]{:S(2)}, u32[]{:S(2)}) %collective-permute-start.5) | collective-permute-done | bytes 28704 | tf_op jit(solution)/shard_map/ppermute | solution.py:28
  17.0 0.4 shard_map.53
  17.4 0.1 collective-permute-start.6
  17.5 2.2 %collective-permute-start.7 = (f32[32,128]{1,0:T(8,128)S(1)}, f32[32,128]{1,0:T(8,128)S(1)}, u32[]{:S(2)}, u32[]{:S(2)}) collective-permute-start(f32[32,128]{1,0:T(8,128)S(1)} %get-tuple-element.30), channel_id=1, source_target_pairs={{0,24},{1,25},{2,26},{3,27},{4,28},{5,29},{6,30},{7,31},{8,16},{9,... | collective-permute-start | bytes 49160 | tf_op jit(solution)/shard_map/ppermute | solution.py:28
  19.7 1.9 %collective-permute-start.8 = (f32[32,128]{1,0:T(8,128)S(1)}, f32[32,128]{1,0:T(8,128)S(1)}, u32[]{:S(2)}, u32[]{:S(2)}) collective-permute-start(f32[32,128]{1,0:T(8,128)S(1)} %get-tuple-element.30), channel_id=1, source_target_pairs={{0,16},{1,17},{2,18},{3,19},{4,20},{5,21},{6,22},{7,23},{8,24},{9,... | collective-permute-start | bytes 49160 | tf_op jit(solution)/shard_map/ppermute | solution.py:28
  21.6 0.0 collective-permute-done.6
  21.6 1.0 %collective-permute-done.7 = f32[32,128]{1,0:T(8,128)S(1)} collective-permute-done((f32[32,128]{1,0:T(8,128)S(1)}, f32[32,128]{1,0:T(8,128)S(1)}, u32[]{:S(2)}, u32[]{:S(2)}) %collective-permute-start.7) | collective-permute-done | bytes 16416 | tf_op jit(solution)/shard_map/ppermute | solution.py:28
  22.5 2.4 %collective-permute-done.8 = f32[32,128]{1,0:T(8,128)S(1)} collective-permute-done((f32[32,128]{1,0:T(8,128)S(1)}, f32[32,128]{1,0:T(8,128)S(1)}, u32[]{:S(2)}, u32[]{:S(2)}) %collective-permute-start.8) | collective-permute-done | bytes 16416 | tf_op jit(solution)/shard_map/ppermute | solution.py:28
  24.9 0.1 collective-permute-start.10
  25.0 5.4 %collective-permute-start.11 = (f32[32,128]{1,0:T(8,128)S(1)}, f32[32,128]{1,0:T(8,128)S(1)}, u32[]{:S(2)}, u32[]{:S(2)}) collective-permute-start(f32[32,128]{1,0:T(8,128)S(1)} %add_add_fusion.1), channel_id=1, source_target_pairs={{0,64},{1,65},{2,66},{3,67},{4,68},{5,69},{6,70},{7,71},{8,72},{9,... | collective-permute-start | bytes 49160 | tf_op jit(solution)/shard_map/ppermute | solution.py:28
  30.4 0.0 collective-permute-start.9
  30.4 0.0 collective-permute-done.10
  30.4 1.9 %collective-permute-done.11 = f32[32,128]{1,0:T(8,128)S(1)} collective-permute-done((f32[32,128]{1,0:T(8,128)S(1)}, f32[32,128]{1,0:T(8,128)S(1)}, u32[]{:S(2)}, u32[]{:S(2)}) %collective-permute-start.11) | collective-permute-done | bytes 16416 | tf_op jit(solution)/shard_map/ppermute | solution.py:28
  32.3 1.9 %collective-permute-done.9 = f32[32,128]{1,0:T(8,128)S(1)} collective-permute-done((f32[32,128]{1,0:T(8,128)S(1)}, f32[32,128]{1,0:T(8,128)S(1)}, u32[]{:S(2)}, u32[]{:S(2)}) %collective-permute-start.9) | collective-permute-done | bytes 16416 | tf_op jit(solution)/shard_map/ppermute | solution.py:28
  34.2 3.1 %collective-permute-start.12 = (f32[32,128]{1,0:T(8,128)S(1)}, f32[32,128]{1,0:T(8,128)S(1)}, u32[]{:S(2)}, u32[]{:S(2)}) collective-permute-start(f32[32,128]{1,0:T(8,128)S(1)} %get-tuple-element.34), channel_id=1, source_target_pairs={{0,224},{1,225},{2,226},{3,227},{4,228},{5,229},{6,230},{7,231},{8... | collective-permute-start | bytes 49160 | tf_op jit(solution)/shard_map/ppermute | solution.py:28
  37.3 1.1 %shard_map.54 = (f32[32,32,128]{2,1,0:T(8,128)S(1)}, f32[32,32,128]{2,1,0:T(8,128)}, f32[32,32,128]{2,1,0:T(8,128)}) custom-call(f32[32,32,128]{2,1,0:T(8,128)S(1)} %get-tuple-element.29.refs_0_, f32[32,128]{1,0:T(8,128)S(1)} %get-tuple-element.35.refs_1_), custom_call_target="tpu_custom_call" | custom-call | flops 2097152 | bytes 2097152 | tf_op jit(solution)/shard_map/pallas_call | solution.py:56
  38.3 2.7 %collective-permute-done.12.refs_2_ = f32[32,128]{1,0:T(8,128)S(1)} collective-permute-done((f32[32,128]{1,0:T(8,128)S(1)}, f32[32,128]{1,0:T(8,128)S(1)}, u32[]{:S(2)}, u32[]{:S(2)}) %collective-permute-start.12) | collective-permute-done | bytes 16416 | tf_op jit(solution)/shard_map/ppermute | solution.py:28
  (8 shorter events, 0.1 us)
Async XLA Ops:
  0.6 12.0 %copy-start = (f32[32,32,128]{2,1,0:T(8,128)S(1)}, f32[32,32,128]{2,1,0:T(8,128)}, u32[]{:S(2)}) copy-start(f32[32,32,128]{2,1,0:T(8,128)} %tracer.3) | copy-start | bytes 1572868
  0.6 12.0 %copy-start.1 = (f32[32,32,128]{2,1,0:T(8,128)S(1)}, f32[32,32,128]{2,1,0:T(8,128)}, u32[]{:S(2)}) copy-start(f32[32,32,128]{2,1,0:T(8,128)} %flow_j.3) | copy-start | bytes 1572868
  0.6 12.0 %copy-start.2 = (f32[32,32,128]{2,1,0:T(8,128)S(1)}, f32[32,32,128]{2,1,0:T(8,128)}, u32[]{:S(2)}) copy-start(f32[32,32,128]{2,1,0:T(8,128)} %flow_i.3) | copy-start | bytes 1572868
  2.2 4.5 %collective-permute-start.2 = (f32[3,16,8,128]{3,2,1,0:T(8,128)S(1)}, f32[3,16,8,128]{3,2,1,0:T(8,128)S(1)}, u32[]{:S(2)}, u32[]{:S(2)}) collective-permute-start(f32[3,16,8,128]{3,2,1,0:T(8,128)S(1)} %get-tuple-element.20), channel_id=1, source_target_pairs={{0,1},{1,0},{2,3},{3,2},{4,5},{5,4},{6,7},{7,6},{8,9},{9,8},{10,11... | collective-permute-start | bytes 589832 | tf_op jit(solution)/shard_map/ppermute | solution.py:28
  2.3 7.1 %collective-permute-start.3 = (f32[3,16,8,128]{3,2,1,0:T(8,128)S(1)}, f32[3,16,8,128]{3,2,1,0:T(8,128)S(1)}, u32[]{:S(2)}, u32[]{:S(2)}) collective-permute-start(f32[3,16,8,128]{3,2,1,0:T(8,128)S(1)} %get-tuple-element.21), channel_id=1, source_target_pairs={{0,8},{1,2},{2,1},{3,4},{4,3},{5,6},{6,5},{7,15},{8,0},{9,10},{10,... | collective-permute-start | bytes 589832 | tf_op jit(solution)/shard_map/ppermute | solution.py:28
  3.8 10.5 %collective-permute-start = (f32[10,32,128]{2,1,0:T(8,128)S(1)}, f32[10,32,128]{2,1,0:T(8,128)S(1)}, u32[]{:S(2)}, u32[]{:S(2)}) collective-permute-start(f32[10,32,128]{2,1,0:T(8,128)S(1)} %get-tuple-element.18), channel_id=1, source_target_pairs={{0,8},{1,9},{2,10},{3,11},{4,12},{5,13},{6,14},{7,15},{8,0},{9,1},... | collective-permute-start | bytes 491528 | tf_op jit(solution)/shard_map/ppermute | solution.py:28
  4.4 10.0 %collective-permute-start.1 = (f32[10,32,128]{2,1,0:T(8,128)S(1)}, f32[10,32,128]{2,1,0:T(8,128)S(1)}, u32[]{:S(2)}, u32[]{:S(2)}) collective-permute-start(f32[10,32,128]{2,1,0:T(8,128)S(1)} %get-tuple-element.19), channel_id=1, source_target_pairs={{0,1},{1,0},{2,3},{3,2},{4,5},{5,4},{6,7},{7,6},{8,16},{9,17},{10,... | collective-permute-start | bytes 491528 | tf_op jit(solution)/shard_map/ppermute | solution.py:28
  9.4 4.9 %collective-permute-start.4 = (f32[7,8,128]{2,1,0:T(8,128)S(1)}, f32[7,8,128]{2,1,0:T(8,128)S(1)}, u32[]{:S(2)}, u32[]{:S(2)}) collective-permute-start(f32[7,8,128]{2,1,0:T(8,128)S(1)} %get-tuple-element.22), channel_id=1, source_target_pairs={{0,8},{1,9},{2,10},{3,11},{4,12},{5,13},{6,14},{7,15},{8,0},{9,1},... | collective-permute-start | bytes 86024 | tf_op jit(solution)/shard_map/ppermute | solution.py:28
  11.0 6.0 %collective-permute-start.5 = (f32[7,8,128]{2,1,0:T(8,128)S(1)}, f32[7,8,128]{2,1,0:T(8,128)S(1)}, u32[]{:S(2)}, u32[]{:S(2)}) collective-permute-start(f32[7,8,128]{2,1,0:T(8,128)S(1)} %get-tuple-element.23), channel_id=1, source_target_pairs={{0,1},{1,0},{2,3},{3,2},{4,5},{5,4},{6,7},{7,6},{8,16},{9,17},{10,... | collective-permute-start | bytes 86024 | tf_op jit(solution)/shard_map/ppermute | solution.py:28
  17.4 4.2 %collective-permute-start.6 = (f32[32,128]{1,0:T(8,128)S(1)}, f32[32,128]{1,0:T(8,128)S(1)}, u32[]{:S(2)}, u32[]{:S(2)}) collective-permute-start(f32[32,128]{1,0:T(8,128)S(1)} %get-tuple-element.30), channel_id=1, source_target_pairs={{0,8},{1,9},{2,10},{3,11},{4,12},{5,13},{6,14},{7,15},{8,0},{9,1},... | collective-permute-start | bytes 49160 | tf_op jit(solution)/shard_map/ppermute | solution.py:28
  17.5 5.0 %collective-permute-start.7 = (f32[32,128]{1,0:T(8,128)S(1)}, f32[32,128]{1,0:T(8,128)S(1)}, u32[]{:S(2)}, u32[]{:S(2)}) collective-permute-start(f32[32,128]{1,0:T(8,128)S(1)} %get-tuple-element.30), channel_id=1, source_target_pairs={{0,24},{1,25},{2,26},{3,27},{4,28},{5,29},{6,30},{7,31},{8,16},{9,... | collective-permute-start | bytes 49160 | tf_op jit(solution)/shard_map/ppermute | solution.py:28
  19.7 5.2 %collective-permute-start.8 = (f32[32,128]{1,0:T(8,128)S(1)}, f32[32,128]{1,0:T(8,128)S(1)}, u32[]{:S(2)}, u32[]{:S(2)}) collective-permute-start(f32[32,128]{1,0:T(8,128)S(1)} %get-tuple-element.30), channel_id=1, source_target_pairs={{0,16},{1,17},{2,18},{3,19},{4,20},{5,21},{6,22},{7,23},{8,24},{9,... | collective-permute-start | bytes 49160 | tf_op jit(solution)/shard_map/ppermute | solution.py:28
  24.9 5.5 %collective-permute-start.10 = (f32[32,128]{1,0:T(8,128)S(1)}, f32[32,128]{1,0:T(8,128)S(1)}, u32[]{:S(2)}, u32[]{:S(2)}) collective-permute-start(f32[32,128]{1,0:T(8,128)S(1)} %add_add_fusion.1), channel_id=1, source_target_pairs={{0,96},{1,97},{2,98},{3,99},{4,100},{5,101},{6,102},{7,103},{8,104... | collective-permute-start | bytes 49160 | tf_op jit(solution)/shard_map/ppermute | solution.py:28
  25.0 7.3 %collective-permute-start.11 = (f32[32,128]{1,0:T(8,128)S(1)}, f32[32,128]{1,0:T(8,128)S(1)}, u32[]{:S(2)}, u32[]{:S(2)}) collective-permute-start(f32[32,128]{1,0:T(8,128)S(1)} %add_add_fusion.1), channel_id=1, source_target_pairs={{0,64},{1,65},{2,66},{3,67},{4,68},{5,69},{6,70},{7,71},{8,72},{9,... | collective-permute-start | bytes 49160 | tf_op jit(solution)/shard_map/ppermute | solution.py:28
  30.4 3.7 %collective-permute-start.9 = (f32[32,128]{1,0:T(8,128)S(1)}, f32[32,128]{1,0:T(8,128)S(1)}, u32[]{:S(2)}, u32[]{:S(2)}) collective-permute-start(f32[32,128]{1,0:T(8,128)S(1)} %add_add_fusion.1), channel_id=1, source_target_pairs={{0,32},{1,33},{2,34},{3,35},{4,36},{5,37},{6,38},{7,39},{8,40},{9,... | collective-permute-start | bytes 49160 | tf_op jit(solution)/shard_map/ppermute | solution.py:28
  34.2 6.8 %collective-permute-start.12 = (f32[32,128]{1,0:T(8,128)S(1)}, f32[32,128]{1,0:T(8,128)S(1)}, u32[]{:S(2)}, u32[]{:S(2)}) collective-permute-start(f32[32,128]{1,0:T(8,128)S(1)} %get-tuple-element.34), channel_id=1, source_target_pairs={{0,224},{1,225},{2,226},{3,227},{4,228},{5,229},{6,230},{7,231},{8... | collective-permute-start | bytes 49160 | tf_op jit(solution)/shard_map/ppermute | solution.py:28

commit v2 on v1

--- a/solution.py
+++ b/solution.py
@@ -92,42 +92,39 @@
         c.wait()
 
 
-def pack_kernel(tracer, flow_j, flow_i, s0, s1, e0, e1, left, right, sems):
+def pack_kernel(tracer, flow_j, flow_i, s0, s1, e0, e1, sems):
     rows, cols = tracer.shape[0], tracer.shape[1]
     even_s, even_e = place_of()[:2]
-    arrays = (tracer, flow_j, flow_i)
-    copies = []
-
-    def copy(src, dst):
-        c = pltpu.make_async_copy(src, dst, sems.at[len(copies)])
-        c.start()
-        copies.append(c)
-
-    for k, a in enumerate(arrays):
-        copy(a.at[:, pl.ds(0, TILE)], left.at[k])
-        copy(a.at[:, pl.ds(cols - TILE, TILE)], right.at[k])
+    half = rows // 2
+    south = []
     at = 0
-    for a, n in zip(arrays, (W, W - 1, W - 1)):
-        high = rows - n
-        copy(a.at[pl.ds(even_s * high, n)], s0.at[pl.ds(at, n)])
-        copy(a.at[pl.ds((1 - even_s) * high, n)], s1.at[pl.ds(at, n)])
+    for k, (a, n) in enumerate(zip((tracer, flow_j, flow_i), (W, W - 1, W - 1))):
+        for m, (dst, edge) in enumerate(((s0, even_s), (s1, 1 - even_s))):
+            src = a.at[pl.ds(edge * (rows - n), n)]
+            south.append(pltpu.make_async_copy(src, dst.at[pl.ds(at, n)], sems.at[2 * k + m]))
         at += n
-    for c in copies[:6]:
-        c.wait()
-    half = rows // 2
-    low = low_half((TILE, tracer.shape[2]))
-
-    def fold(j, carry):
-        for k in range(3):
-            lo = jnp.where(low, left[k, j], pltpu.roll(left[k, j + half], W, 0))
-            hi = jnp.where(low, pltpu.roll(right[k, j], W, 0), right[k, j + half])
-            e0[k, j] = jnp.where(even_e == 1, hi, lo)
-            e1[k, j] = jnp.where(even_e == 1, lo, hi)
-        return carry
-
-    lax.fori_loop(0, half, fold, 0, unroll=4)
-    for c in copies[6:]:
-        c.wait()
+
+    def fold(right, left):
+        copies = []
+        for k, a in enumerate((tracer, flow_j, flow_i)):
+            for m, (dst, column) in enumerate(((right, cols - W), (left, 0))):
+                for h in range(2):
+                    src = a.at[pl.ds(h * half, half), pl.ds(column, W)]
+                    to = dst.at[k, :, pl.ds(h * W, W)]
+                    copies.append(pltpu.make_async_copy(src, to, sems.at[6 + 4 * k + 2 * m + h]))
+        start_all(copies)
+        start_all(south)
+        wait_all(copies)
+
+    @pl.when(even_e == 1)
+    def _():
+        fold(e0, e1)
+
+    @pl.when(even_e == 0)
+    def _():
+        fold(e1, e0)
+
+    wait_all(south)
 
 
 def unfolded(e0, e1, k, j):
@@ -307,8 +304,9 @@
     fold = (3, rows // 2, TILE, members)
     s0, s1, e0, e1 = call(
         pack_kernel, (edge, edge, fold, fold), fields, [HBM] * 3,
-        [pltpu.VMEM((3, rows, TILE, members), jnp.float32)] * 2 + [pltpu.SemaphoreType.DMA((12,))],
-    )
+        [pltpu.SemaphoreType.DMA((18,))],
+    )
+    later = lax.optimization_barrier((tracer, flow_j, flow_i, e1))[:3]
     e1 = exchange(e1, east_odd)
     e0 = exchange(e0, east_even)
     s1 = exchange(s1, south_odd)
@@ -323,7 +321,7 @@
     ends = (STEPS, 2, 2, cols + TILE, members)
     inner = call(
         inner_kernel, (wide, wide, ends, tracer.shape, (cols, members)),
-        (tracer, flow_j, flow_i, e0, e1), [ANY] * 3 + [VMEM] * 2,
+        (*later, e0, e1), [ANY] * 3 + [VMEM] * 2,
         [pltpu.VMEM(wide, jnp.float32), pltpu.SemaphoreType.DMA((3,))], cost=1 << 22,
     )
     end, total = call(

time: 41.1 us -> 40.9 us (level)
  waiting for transfers between devices: 15.1 us -> 14.5 us
  starting transfers between devices: 20.5 us -> 21 us
    ppermute x13, waiting for transfers between devices: 15.1 us -> 14.5 us  [exchange(): return lax.ppermute(array, ('south', 'east'), pairs)]
    ppermute x13, starting transfers between devices: 20.5 us -> 21 us  [exchange(): return lax.ppermute(array, ('south', 'east'), pairs)]
where the time goes in v2:
time: 40.9 us; the launch traced here: 40.8 us
  starting transfers between devices  21 us (51%)
  waiting for transfers between devices  14.5 us (35%)
  Pallas kernels  4.58 us (11%)
  between operations  0.73 us (2%)
    ppermute x13, starting transfers between devices, exchange(): return lax.ppermute(array, ('south', 'east'), pairs)  21 us
    ppermute x13, waiting for transfers between devices, exchange(): return lax.ppermute(array, ('south', 'east'), pairs)  14.5 us
    pallas_call x6, Pallas kernels, call(): pl.pallas_call(kernel, out_shape=tuple(((jax.ShapeDtypeStruct if i in res...  4.58 us
  transfers between devices with their start and end apart: 13, of which 7 were waited for; matrix products, arithmetic and copies ran while one was open for 0% of the time, Pallas kernels for 7%

profile of v2, /device:TPU:64, one launch (start us, length us, event | category | flops | bytes accessed | tf_op | source)
XLA Modules:
  0.0 40.8 jit_solution(15220755385937938910)
XLA Ops:
  0.6 0.0 copy-start
  0.6 0.0 copy-start.1
  0.7 1.4 %shard_map.50 = (f32[10,32,128]{2,1,0:T(8,128)S(1)}, f32[10,32,128]{2,1,0:T(8,128)S(1)}, f32[3,16,8,128]{3,2,1,0:T(8,128)S(1)}, f32[3,16,8,128]{3,2,1,0:T(8,128)S(1)}) custom-call(f32[32,32,128]{2,1,0:T(8,128)} %tracer.2, f32[32,32,128]{2,1,0:T(8,128)} %flow_j.2, f32[32,32,128]{2,1,0:T(8,128)} %flow_i.2), custom_call_target="tpu_custom_call" | custom-call | tf_op jit(solution)/shard_map/pallas_call | solution.py:56
  2.1 1.6 %collective-permute-start.3 = (f32[3,16,8,128]{3,2,1,0:T(8,128)S(1)}, f32[3,16,8,128]{3,2,1,0:T(8,128)S(1)}, u32[]{:S(2)}, u32[]{:S(2)}) collective-permute-start(f32[3,16,8,128]{3,2,1,0:T(8,128)S(1)} %get-tuple-element.24), channel_id=1, source_target_pairs={{0,8},{1,2},{2,1},{3,4},{4,3},{5,6},{6,5},{7,15},{8,0},{9,10},{10,... | collective-permute-start | bytes 589832 | tf_op jit(solution)/shard_map/ppermute | solution.py:28
  3.6 0.2 collective-permute-start.2
  3.8 1.5 %collective-permute-start = (f32[10,32,128]{2,1,0:T(8,128)S(1)}, f32[10,32,128]{2,1,0:T(8,128)S(1)}, u32[]{:S(2)}, u32[]{:S(2)}) collective-permute-start(f32[10,32,128]{2,1,0:T(8,128)S(1)} %get-tuple-element.21), channel_id=1, source_target_pairs={{0,8},{1,9},{2,10},{3,11},{4,12},{5,13},{6,14},{7,15},{8,0},{9,1},... | collective-permute-start | bytes 491528 | tf_op jit(solution)/shard_map/ppermute | solution.py:28
  5.3 1.6 %collective-permute-start.1 = (f32[10,32,128]{2,1,0:T(8,128)S(1)}, f32[10,32,128]{2,1,0:T(8,128)S(1)}, u32[]{:S(2)}, u32[]{:S(2)}) collective-permute-start(f32[10,32,128]{2,1,0:T(8,128)S(1)} %get-tuple-element.22), channel_id=1, source_target_pairs={{0,1},{1,0},{2,3},{3,2},{4,5},{5,4},{6,7},{7,6},{8,16},{9,17},{10,... | collective-permute-start | bytes 491528 | tf_op jit(solution)/shard_map/ppermute | solution.py:28
  7.0 1.9 %collective-permute-done.3.e1 = f32[3,16,8,128]{3,2,1,0:T(8,128)S(1)} collective-permute-done((f32[3,16,8,128]{3,2,1,0:T(8,128)S(1)}, f32[3,16,8,128]{3,2,1,0:T(8,128)S(1)}, u32[]{:S(2)}, u32[]{:S(2)}) %collective-permute-start.3) | collective-permute-done | bytes 196640 | tf_op jit(solution)/shard_map/ppermute | solution.py:28
  8.9 0.0 collective-permute-done.2.e0
  8.9 1.9 %collective-permute-start.4 = (f32[7,8,128]{2,1,0:T(8,128)S(1)}, f32[7,8,128]{2,1,0:T(8,128)S(1)}, u32[]{:S(2)}, u32[]{:S(2)}) collective-permute-start(f32[7,8,128]{2,1,0:T(8,128)S(1)} %get-tuple-element.25), channel_id=1, source_target_pairs={{0,8},{1,9},{2,10},{3,11},{4,12},{5,13},{6,14},{7,15},{8,0},{9,1},... | collective-permute-start | bytes 86024 | tf_op jit(solution)/shard_map/ppermute | solution.py:28
  10.8 1.6 %collective-permute-start.5 = (f32[7,8,128]{2,1,0:T(8,128)S(1)}, f32[7,8,128]{2,1,0:T(8,128)S(1)}, u32[]{:S(2)}, u32[]{:S(2)}) collective-permute-start(f32[7,8,128]{2,1,0:T(8,128)S(1)} %get-tuple-element.26), channel_id=1, source_target_pairs={{0,1},{1,0},{2,3},{3,2},{4,5},{5,4},{6,7},{7,6},{8,16},{9,17},{10,... | collective-permute-start | bytes 86024 | tf_op jit(solution)/shard_map/ppermute | solution.py:28
  12.4 1.7 %shard_map.52 = (f32[32,40,128]{2,1,0:T(8,128)S(1)}, f32[32,40,128]{2,1,0:T(8,128)S(1)}, f32[4,2,2,40,128]{4,3,2,1,0:T(8,128)S(1)}, f32[32,32,128]{2,1,0:T(8,128)S(1)}, f32[32,128]{1,0:T(8,128)S(1)}) custom-call(f32[32,32,128]{2,1,0:T(8,128)S(1)} %copy-done, f32[32,32,128]{2,1,0:T(8,128)S(1)} %copy-done.1, f32[32,32,128]{2,1,0:T(8,128)S(1)} %copy-done.2, ...), custom_call_target="tpu_custom_call" | custom-call | flops 4194304 | bytes 4194304 | tf_op jit(solution)/shard_map/pallas_call | solution.py:56
  14.1 0.0 collective-permute-done.recv0
  14.1 0.0 collective-permute-done.1.recv1
  14.1 0.0 collective-permute-done.4.corner0
  14.1 2.6 %collective-permute-done.5.corner1 = f32[7,8,128]{2,1,0:T(8,128)S(1)} collective-permute-done((f32[7,8,128]{2,1,0:T(8,128)S(1)}, f32[7,8,128]{2,1,0:T(8,128)S(1)}, u32[]{:S(2)}, u32[]{:S(2)}) %collective-permute-start.5) | collective-permute-done | bytes 28704 | tf_op jit(solution)/shard_map/ppermute | solution.py:28
  16.8 0.4 shard_map.53
  17.2 0.1 collective-permute-start.6
  17.3 2.2 %collective-permute-start.7 = (f32[32,128]{1,0:T(8,128)S(1)}, f32[32,128]{1,0:T(8,128)S(1)}, u32[]{:S(2)}, u32[]{:S(2)}) collective-permute-start(f32[32,128]{1,0:T(8,128)S(1)} %get-tuple-element.36), channel_id=1, source_target_pairs={{0,24},{1,25},{2,26},{3,27},{4,28},{5,29},{6,30},{7,31},{8,16},{9,... | collective-permute-start | bytes 49160 | tf_op jit(solution)/shard_map/ppermute | solution.py:28
  19.5 1.9 %collective-permute-start.8 = (f32[32,128]{1,0:T(8,128)S(1)}, f32[32,128]{1,0:T(8,128)S(1)}, u32[]{:S(2)}, u32[]{:S(2)}) collective-permute-start(f32[32,128]{1,0:T(8,128)S(1)} %get-tuple-element.36), channel_id=1, source_target_pairs={{0,16},{1,17},{2,18},{3,19},{4,20},{5,21},{6,22},{7,23},{8,24},{9,... | collective-permute-start | bytes 49160 | tf_op jit(solution)/shard_map/ppermute | solution.py:28
  21.4 0.0 collective-permute-done.6
  21.4 1.0 %collective-permute-done.7 = f32[32,128]{1,0:T(8,128)S(1)} collective-permute-done((f32[32,128]{1,0:T(8,128)S(1)}, f32[32,128]{1,0:T(8,128)S(1)}, u32[]{:S(2)}, u32[]{:S(2)}) %collective-permute-start.7) | collective-permute-done | bytes 16416 | tf_op jit(solution)/shard_map/ppermute | solution.py:28
  22.3 2.4 %collective-permute-done.8 = f32[32,128]{1,0:T(8,128)S(1)} collective-permute-done((f32[32,128]{1,0:T(8,128)S(1)}, f32[32,128]{1,0:T(8,128)S(1)}, u32[]{:S(2)}, u32[]{:S(2)}) %collective-permute-start.8) | collective-permute-done | bytes 16416 | tf_op jit(solution)/shard_map/ppermute | solution.py:28
  24.7 0.1 collective-permute-start.10
  24.8 5.4 %collective-permute-start.11 = (f32[32,128]{1,0:T(8,128)S(1)}, f32[32,128]{1,0:T(8,128)S(1)}, u32[]{:S(2)}, u32[]{:S(2)}) collective-permute-start(f32[32,128]{1,0:T(8,128)S(1)} %add_add_fusion.1), channel_id=1, source_target_pairs={{0,64},{1,65},{2,66},{3,67},{4,68},{5,69},{6,70},{7,71},{8,72},{9,... | collective-permute-start | bytes 49160 | tf_op jit(solution)/shard_map/ppermute | solution.py:28
  30.2 0.0 collective-permute-start.9
  30.2 0.0 collective-permute-done.10
  30.2 1.9 %collective-permute-done.11 = f32[32,128]{1,0:T(8,128)S(1)} collective-permute-done((f32[32,128]{1,0:T(8,128)S(1)}, f32[32,128]{1,0:T(8,128)S(1)}, u32[]{:S(2)}, u32[]{:S(2)}) %collective-permute-start.11) | collective-permute-done | bytes 16416 | tf_op jit(solution)/shard_map/ppermute | solution.py:28
  32.1 1.9 %collective-permute-done.9 = f32[32,128]{1,0:T(8,128)S(1)} collective-permute-done((f32[32,128]{1,0:T(8,128)S(1)}, f32[32,128]{1,0:T(8,128)S(1)}, u32[]{:S(2)}, u32[]{:S(2)}) %collective-permute-start.9) | collective-permute-done | bytes 16416 | tf_op jit(solution)/shard_map/ppermute | solution.py:28
  34.0 2.9 %collective-permute-start.12 = (f32[32,128]{1,0:T(8,128)S(1)}, f32[32,128]{1,0:T(8,128)S(1)}, u32[]{:S(2)}, u32[]{:S(2)}) collective-permute-start(f32[32,128]{1,0:T(8,128)S(1)} %get-tuple-element.40), channel_id=1, source_target_pairs={{0,224},{1,225},{2,226},{3,227},{4,228},{5,229},{6,230},{7,231},{8... | collective-permute-start | bytes 49160 | tf_op jit(solution)/shard_map/ppermute | solution.py:28
  36.9 1.1 %shard_map.54 = (f32[32,32,128]{2,1,0:T(8,128)S(1)}, f32[32,32,128]{2,1,0:T(8,128)}, f32[32,32,128]{2,1,0:T(8,128)}) custom-call(f32[32,32,128]{2,1,0:T(8,128)S(1)} %get-tuple-element.35.refs_0_, f32[32,128]{1,0:T(8,128)S(1)} %get-tuple-element.41.refs_1_), custom_call_target="tpu_custom_call" | custom-call | flops 2097152 | bytes 2097152 | tf_op jit(solution)/shard_map/pallas_call | solution.py:56
  37.9 2.8 %collective-permute-done.12.refs_2_ = f32[32,128]{1,0:T(8,128)S(1)} collective-permute-done((f32[32,128]{1,0:T(8,128)S(1)}, f32[32,128]{1,0:T(8,128)S(1)}, u32[]{:S(2)}, u32[]{:S(2)}) %collective-permute-start.12) | collective-permute-done | bytes 16416 | tf_op jit(solution)/shard_map/ppermute | solution.py:28
  (8 shorter events, 0.1 us)
Async XLA Ops:
  0.6 11.8 %copy-start = (f32[32,32,128]{2,1,0:T(8,128)S(1)}, f32[32,32,128]{2,1,0:T(8,128)}, u32[]{:S(2)}) copy-start(f32[32,32,128]{2,1,0:T(8,128)} %tracer.2) | copy-start | bytes 1572868
  0.6 11.8 %copy-start.1 = (f32[32,32,128]{2,1,0:T(8,128)S(1)}, f32[32,32,128]{2,1,0:T(8,128)}, u32[]{:S(2)}) copy-start(f32[32,32,128]{2,1,0:T(8,128)} %flow_j.2) | copy-start | bytes 1572868
  0.6 11.8 %copy-start.2 = (f32[32,32,128]{2,1,0:T(8,128)S(1)}, f32[32,32,128]{2,1,0:T(8,128)}, u32[]{:S(2)}) copy-start(f32[32,32,128]{2,1,0:T(8,128)} %flow_i.2) | copy-start | bytes 1572868
  2.1 6.8 %collective-permute-start.3 = (f32[3,16,8,128]{3,2,1,0:T(8,128)S(1)}, f32[3,16,8,128]{3,2,1,0:T(8,128)S(1)}, u32[]{:S(2)}, u32[]{:S(2)}) collective-permute-start(f32[3,16,8,128]{3,2,1,0:T(8,128)S(1)} %get-tuple-element.24), channel_id=1, source_target_pairs={{0,8},{1,2},{2,1},{3,4},{4,3},{5,6},{6,5},{7,15},{8,0},{9,10},{10,... | collective-permute-start | bytes 589832 | tf_op jit(solution)/shard_map/ppermute | solution.py:28
  3.6 5.3 %collective-permute-start.2 = (f32[3,16,8,128]{3,2,1,0:T(8,128)S(1)}, f32[3,16,8,128]{3,2,1,0:T(8,128)S(1)}, u32[]{:S(2)}, u32[]{:S(2)}) collective-permute-start(f32[3,16,8,128]{3,2,1,0:T(8,128)S(1)} %get-tuple-element.23), channel_id=1, source_target_pairs={{0,1},{1,0},{2,3},{3,2},{4,5},{5,4},{6,7},{7,6},{8,9},{9,8},{10,11... | collective-permute-start | bytes 589832 | tf_op jit(solution)/shard_map/ppermute | solution.py:28
  3.8 10.3 %collective-permute-start = (f32[10,32,128]{2,1,0:T(8,128)S(1)}, f32[10,32,128]{2,1,0:T(8,128)S(1)}, u32[]{:S(2)}, u32[]{:S(2)}) collective-permute-start(f32[10,32,128]{2,1,0:T(8,128)S(1)} %get-tuple-element.21), channel_id=1, source_target_pairs={{0,8},{1,9},{2,10},{3,11},{4,12},{5,13},{6,14},{7,15},{8,0},{9,1},... | collective-permute-start | bytes 491528 | tf_op jit(solution)/shard_map/ppermute | solution.py:28
  5.3 8.8 %collective-permute-start.1 = (f32[10,32,128]{2,1,0:T(8,128)S(1)}, f32[10,32,128]{2,1,0:T(8,128)S(1)}, u32[]{:S(2)}, u32[]{:S(2)}) collective-permute-start(f32[10,32,128]{2,1,0:T(8,128)S(1)} %get-tuple-element.22), channel_id=1, source_target_pairs={{0,1},{1,0},{2,3},{3,2},{4,5},{5,4},{6,7},{7,6},{8,16},{9,17},{10,... | collective-permute-start | bytes 491528 | tf_op jit(solution)/shard_map/ppermute | solution.py:28
  8.9 5.2 %collective-permute-start.4 = (f32[7,8,128]{2,1,0:T(8,128)S(1)}, f32[7,8,128]{2,1,0:T(8,128)S(1)}, u32[]{:S(2)}, u32[]{:S(2)}) collective-permute-start(f32[7,8,128]{2,1,0:T(8,128)S(1)} %get-tuple-element.25), channel_id=1, source_target_pairs={{0,8},{1,9},{2,10},{3,11},{4,12},{5,13},{6,14},{7,15},{8,0},{9,1},... | collective-permute-start | bytes 86024 | tf_op jit(solution)/shard_map/ppermute | solution.py:28
  10.8 6.0 %collective-permute-start.5 = (f32[7,8,128]{2,1,0:T(8,128)S(1)}, f32[7,8,128]{2,1,0:T(8,128)S(1)}, u32[]{:S(2)}, u32[]{:S(2)}) collective-permute-start(f32[7,8,128]{2,1,0:T(8,128)S(1)} %get-tuple-element.26), channel_id=1, source_target_pairs={{0,1},{1,0},{2,3},{3,2},{4,5},{5,4},{6,7},{7,6},{8,16},{9,17},{10,... | collective-permute-start | bytes 86024 | tf_op jit(solution)/shard_map/ppermute | solution.py:28
  17.2 4.2 %collective-permute-start.6 = (f32[32,128]{1,0:T(8,128)S(1)}, f32[32,128]{1,0:T(8,128)S(1)}, u32[]{:S(2)}, u32[]{:S(2)}) collective-permute-start(f32[32,128]{1,0:T(8,128)S(1)} %get-tuple-element.36), channel_id=1, source_target_pairs={{0,8},{1,9},{2,10},{3,11},{4,12},{5,13},{6,14},{7,15},{8,0},{9,1},... | collective-permute-start | bytes 49160 | tf_op jit(solution)/shard_map/ppermute | solution.py:28
  17.3 5.0 %collective-permute-start.7 = (f32[32,128]{1,0:T(8,128)S(1)}, f32[32,128]{1,0:T(8,128)S(1)}, u32[]{:S(2)}, u32[]{:S(2)}) collective-permute-start(f32[32,128]{1,0:T(8,128)S(1)} %get-tuple-element.36), channel_id=1, source_target_pairs={{0,24},{1,25},{2,26},{3,27},{4,28},{5,29},{6,30},{7,31},{8,16},{9,... | collective-permute-start | bytes 49160 | tf_op jit(solution)/shard_map/ppermute | solution.py:28
  19.5 5.2 %collective-permute-start.8 = (f32[32,128]{1,0:T(8,128)S(1)}, f32[32,128]{1,0:T(8,128)S(1)}, u32[]{:S(2)}, u32[]{:S(2)}) collective-permute-start(f32[32,128]{1,0:T(8,128)S(1)} %get-tuple-element.36), channel_id=1, source_target_pairs={{0,16},{1,17},{2,18},{3,19},{4,20},{5,21},{6,22},{7,23},{8,24},{9,... | collective-permute-start | bytes 49160 | tf_op jit(solution)/shard_map/ppermute | solution.py:28
  24.7 5.5 %collective-permute-start.10 = (f32[32,128]{1,0:T(8,128)S(1)}, f32[32,128]{1,0:T(8,128)S(1)}, u32[]{:S(2)}, u32[]{:S(2)}) collective-permute-start(f32[32,128]{1,0:T(8,128)S(1)} %add_add_fusion.1), channel_id=1, source_target_pairs={{0,96},{1,97},{2,98},{3,99},{4,100},{5,101},{6,102},{7,103},{8,104... | collective-permute-start | bytes 49160 | tf_op jit(solution)/shard_map/ppermute | solution.py:28
  24.8 7.3 %collective-permute-start.11 = (f32[32,128]{1,0:T(8,128)S(1)}, f32[32,128]{1,0:T(8,128)S(1)}, u32[]{:S(2)}, u32[]{:S(2)}) collective-permute-start(f32[32,128]{1,0:T(8,128)S(1)} %add_add_fusion.1), channel_id=1, source_target_pairs={{0,64},{1,65},{2,66},{3,67},{4,68},{5,69},{6,70},{7,71},{8,72},{9,... | collective-permute-start | bytes 49160 | tf_op jit(solution)/shard_map/ppermute | solution.py:28
  30.2 3.7 %collective-permute-start.9 = (f32[32,128]{1,0:T(8,128)S(1)}, f32[32,128]{1,0:T(8,128)S(1)}, u32[]{:S(2)}, u32[]{:S(2)}) collective-permute-start(f32[32,128]{1,0:T(8,128)S(1)} %add_add_fusion.1), channel_id=1, source_target_pairs={{0,32},{1,33},{2,34},{3,35},{4,36},{5,37},{6,38},{7,39},{8,40},{9,... | collective-permute-start | bytes 49160 | tf_op jit(solution)/shard_map/ppermute | solution.py:28
  34.0 6.8 %collective-permute-start.12 = (f32[32,128]{1,0:T(8,128)S(1)}, f32[32,128]{1,0:T(8,128)S(1)}, u32[]{:S(2)}, u32[]{:S(2)}) collective-permute-start(f32[32,128]{1,0:T(8,128)S(1)} %get-tuple-element.40), channel_id=1, source_target_pairs={{0,224},{1,225},{2,226},{3,227},{4,228},{5,229},{6,230},{7,231},{8... | collective-permute-start | bytes 49160 | tf_op jit(solution)/shard_map/ppermute | solution.py:28
